TPU v7x, 32 devices: a whole 2x2x4 slice. The times are simulated.
32 devices in a mesh: tm: 4 (over z), env: 8 (over y, x, core).
Axes of the slice: x: 2, y: 2, z: 4, core: 2. Of those that a mesh axis runs over, the one named last changes fastest.
Arguments:
- rewards: float32 [1024, 1024], P('tm', 'env'), may hold values from -6 to 6
- dones: int32 [1024, 1024], P('tm', 'env'), may hold values 0 or 1
- horizon: float32 [1024], P('env'), may hold values from 20 to 2048
- bootstrap: float32 [1024], P('env'), may hold values from -96 to 96
- prior_mean: float32 [1], replicated, may hold values from -240 to 240
- prior_var: float32 [1], replicated, may hold values from 100 to 3000
Outputs:
- scaled_rewards: float32 [1024, 1024], P('tm', 'env')
- scaled_returns: float32 [1024, 1024], P('tm', 'env')
- running_stats: float32 [2], replicated
All inputs are finite; a program needn't handle non-finite values. No bound on the sum of `dones` on one device may be relied on, other than what follows from the above.
Results may differ from a plain program's by a relative error of at most 0.0003.
Values sent between devices are 32-bit elements; how exact they have to be, the bound alone decides.
A program may use at most 64 MiB of HBM per device.

v0:
```python
import functools

import jax
import jax.numpy as jnp
from jax import lax
from jax.experimental import pallas as pl
from jax.experimental.pallas import tpu as pltpu
from jax.sharding import PartitionSpec as P

SUB = 8
ROWS = 8
SENT = 7
PARTS = 2


def compose_rows(summed, product, row):
    step = 1
    while step < SUB:
        inside = row < SUB - step
        later_sum = jnp.where(inside, pltpu.roll(summed, SUB - step, 0), 0.0)
        later_product = jnp.where(inside, pltpu.roll(product, SUB - step, 0), 1.0)
        summed = summed + product * later_sum
        product = product * later_product
        step *= 2
    return summed, product


def kernel(T, E, rewards_hbm, dones_hbm, horizon_hbm, bootstrap_hbm, mean_hbm, var_hbm,
           rewards, s_buf, p_buf, carry_ref, ebuf, prior_ref,
           dones, horizon_ref, bootstrap_ref, mean_ref, var_ref, tbuf, xbuf,
           load_sem, tsend, trecv):
    t = lax.axis_index("tm")
    e = lax.axis_index("env")
    barrier = pltpu.get_barrier_semaphore()
    offsets = [(i, j) for i in range(T) for j in range(E) if i or j]
    offsets.sort(key=lambda o: -min(o[0], T - o[0]))
    peers = [{"tm": lax.rem(t + i, T), "env": lax.rem(e + j, E)} for i, j in offsets]
    for peer in peers:
        pl.semaphore_signal(barrier, inc=1, device_id=peer, device_id_type=pl.DeviceIdType.MESH)
    pairs = [(horizon_hbm, horizon_ref), (mean_hbm, mean_ref), (var_hbm, var_ref),
             (bootstrap_hbm, bootstrap_ref), (rewards_hbm, rewards),
             (dones_hbm, dones)]
    loads = [pltpu.make_async_copy(source, target, load_sem.at[i])
             for i, (source, target) in enumerate(pairs)]
    for load in loads:
        load.start()
    rows, lanes = rewards.shape
    chunk = rows // SUB
    shape = (SUB, lanes)
    row = lax.broadcasted_iota(jnp.int32, shape, 0)
    for load in loads:
        load.wait()
    discount = jnp.broadcast_to(1.0 - 1.0 / horizon_ref[...], shape)
    center = jnp.full(shape, mean_ref[0], jnp.float32)
    s = jnp.zeros(shape, jnp.float32)
    p = jnp.ones(shape, jnp.float32)
    zero = jnp.zeros(shape, jnp.float32)
    s1, p1, s2, sp, p2 = zero, zero, zero, zero, zero
    for k in reversed(range(chunk)):
        r = rewards[pl.ds(k, SUB, stride=chunk), :]
        f = jnp.where(dones[pl.ds(k, SUB, stride=chunk), :] == 0, discount, 0.0)
        s = r + f * s
        p = f * p
        s_buf[k] = s
        p_buf[k] = p
        c = s - center
        s1 = s1 + c
        p1 = p1 + p
        s2 = s2 + c * c
        sp = sp + c * p
        p2 = p2 + p * p
    full_s, full_p = compose_rows(s, p, row)
    last = row == SUB - 1
    a = jnp.where(last, 0.0, pltpu.roll(full_s, SUB - 1, 0))
    b = jnp.where(last, 1.0, pltpu.roll(full_p, SUB - 1, 0))
    down = lambda value: jnp.sum(value, axis=0, keepdims=True)
    known = jnp.where(t == T - 1, bootstrap_ref[...], jnp.zeros((1, lanes), jnp.float32))
    a = a + b * known
    rest = sp + a * p2
    tbuf[t, e, 0:1] = full_s[0:1] + full_p[0:1] * known
    tbuf[t, e, 1:2] = full_p[0:1]
    tbuf[t, e, 2:3] = down(s1 + p1 * a)
    tbuf[t, e, 3:4] = down(p1 * b)
    tbuf[t, e, 4:5] = down(s2 + a * (sp + rest))
    tbuf[t, e, 5:6] = down(2.0 * b * rest)
    tbuf[t, e, 6:7] = down(b * b * p2)
    pl.semaphore_wait(barrier, T * E - 1)
    copies = [pltpu.make_async_remote_copy(
        tbuf.at[t, e, 0:SENT], tbuf.at[t, e, 0:SENT], tsend.at[i], trecv.at[i],
        device_id=peer, device_id_type=pl.DeviceIdType.MESH) for i, peer in enumerate(peers)]
    for copy in copies:
        copy.start()
    for copy in copies:
        copy.wait()
    x = jnp.zeros((E, lanes), jnp.float32)
    first = jnp.zeros((E, lanes), jnp.float32)
    second = jnp.zeros((E, lanes), jnp.float32)
    for j in reversed(range(T)):
        xbuf[j] = x
        first = first + tbuf[j, :, 2] + tbuf[j, :, 3] * x
        second = second + tbuf[j, :, 4] + x * (tbuf[j, :, 5] + x * tbuf[j, :, 6])
        x = tbuf[j, :, 0] + tbuf[j, :, 1] * x
    mine = xbuf[t, pl.ds(e, 1), :]
    ebuf[0] = first
    ebuf[1] = second
    prior_ref[0:1] = center[0:1]
    prior_ref[1:2] = jnp.full((1, lanes), var_ref[0], jnp.float32)
    carry_ref[...] = a + b * mine


def finish(T, E, rewards, s_buf, p_buf, carry_ref, ebuf, prior_ref, out_rewards, out_returns, out_stats,
           rewards_out, returns_out, stats, sems):
    rows, lanes = rewards.shape
    chunk = rows // SUB
    first = jnp.sum(jnp.sum(ebuf[0], axis=0, keepdims=True), axis=1, keepdims=True)
    second = jnp.sum(jnp.sum(ebuf[1], axis=0, keepdims=True), axis=1, keepdims=True)
    entries = float(rows * T * lanes * E)
    prior_count = entries
    merged = prior_count + entries
    mean0 = prior_ref[0:1, 0:1]
    var0 = prior_ref[1:2, 0:1]
    delta = first * (1.0 / entries)
    spread = second - first * delta
    new_mean = mean0 + delta * (entries / merged)
    variance = (var0 * (prior_count / merged) + spread * (1.0 / merged)
                + delta * delta * (prior_count / merged * (entries / merged)))
    inverse = jnp.broadcast_to(lax.rsqrt(variance + 1e-08), (SUB, lanes))
    copies = []

    def send(source, target, rank):
        copy = pltpu.make_async_copy(source, target, sems.at[rank])
        copy.start()
        copies.append(copy)

    y = carry_ref[...] * inverse
    for k in range(chunk):
        returns_out[pl.ds(k, SUB, stride=chunk), :] = s_buf[k] * inverse + p_buf[k] * y
    send(returns_out, out_returns, 0)
    part = rows // PARTS
    for i in range(PARTS):
        for k in range(i * part, (i + 1) * part, SUB):
            rewards_out[k:k + SUB] = rewards[k:k + SUB] * inverse
        where = pl.ds(i * part, part)
        send(rewards_out.at[where], out_rewards.at[where], 2 + i)
    stats[0] = new_mean[0, 0]
    stats[1] = variance[0, 0]
    send(stats, out_stats, 1)
    for copy in copies:
        copy.wait()


def local(T, E, rewards, dones, horizon, bootstrap, prior_mean, prior_var):
    rows, lanes = rewards.shape
    block = (rows, lanes)
    vmem = pl.BlockSpec(memory_space=pltpu.VMEM)
    hbm = pl.BlockSpec(memory_space=pltpu.HBM)
    kept, summed, product, carry, sums, prior = pl.pallas_call(
        functools.partial(kernel, T, E),
        out_shape=(pltpu.VMEM(block, jnp.float32),
                   pltpu.VMEM((rows // SUB, SUB, lanes), jnp.float32),
                   pltpu.VMEM((rows // SUB, SUB, lanes), jnp.float32),
                   pltpu.VMEM((SUB, lanes), jnp.float32),
                   pltpu.VMEM((2, E, lanes), jnp.float32), pltpu.VMEM((2, lanes), jnp.float32)),
        in_specs=[hbm] * 6,
        out_specs=(vmem,) * 6,
        scratch_shapes=[
            pltpu.VMEM(block, jnp.int32),
            pltpu.VMEM((1, lanes), jnp.float32),
            pltpu.VMEM((1, lanes), jnp.float32),
            pltpu.SMEM((1,), jnp.float32),
            pltpu.SMEM((1,), jnp.float32),
            pltpu.VMEM((T, E, ROWS, lanes), jnp.float32),
            pltpu.VMEM((T, E, lanes), jnp.float32),
            pltpu.SemaphoreType.DMA((6,)),
            pltpu.SemaphoreType.DMA((T * E - 1,)),
            pltpu.SemaphoreType.DMA((T * E - 1,)),
        ],
        compiler_params=pltpu.CompilerParams(collective_id=0, has_side_effects=True),
    )(rewards, dones, horizon.reshape(1, lanes), bootstrap.reshape(1, lanes), prior_mean, prior_var)
    return pl.pallas_call(
        functools.partial(finish, T, E),
        out_shape=(jax.ShapeDtypeStruct(block, jnp.float32),
                   jax.ShapeDtypeStruct(block, jnp.float32),
                   jax.ShapeDtypeStruct((2,), jnp.float32)),
        in_specs=[vmem] * 6,
        out_specs=(hbm, hbm, hbm),
        scratch_shapes=[
            pltpu.VMEM(block, jnp.float32),
            pltpu.VMEM(block, jnp.float32),
            pltpu.SMEM((2,), jnp.float32),
            pltpu.SemaphoreType.DMA((2 + PARTS,)),
        ],
        compiler_params=pltpu.CompilerParams(vmem_limit_bytes=4 * 2**20),
    )(kept, summed, product, carry, sums, prior)


def solution(mesh):
    T, E = mesh.shape["tm"], mesh.shape["env"]
    return jax.shard_map(
        functools.partial(local, T, E),
        mesh=mesh,
        in_specs=(P("tm", "env"), P("tm", "env"), P("env"), P("env"), P(), P()),
        out_specs=(P("tm", "env"), P("tm", "env"), P()),
        check_vma=False,
    )
```

profile of v0, /device:TPU:0, one launch (start us, length us, event | category | flops | bytes accessed | tf_op | source)
XLA Modules:
  0.0 14.2 jit_solution(4856736181771444968)
XLA Ops:
  1.9 11.3 %shard_map.85 = (f32[256,128]{1,0:T(8,128)S(1)}, f32[32,8,128]{2,1,0:T(8,128)S(1)}, f32[32,8,128]{2,1,0:T(8,128)S(1)}, f32[8,128]{1,0:T(8,128)S(1)}, f32[2,8,128]{2,1,0:T(8,128)S(1)}, /*index=5*/f32[2,128]{1,0:T(2,128)S(1)}) custom-call(f32[256,128]{1,0:T(8,128)} %rewards_hbm.1, s32[256,128]{1,0:T(8,128)} %dones_hbm.1, f32[1,128]{1,0:T(1,128)} %bitcast.2, ...), custom_call_target="tpu_custom_call" | custom-call | tf_op jit(solution)/shard_map/pallas_call | solution.py:157
  13.2 1.0 %shard_map.86 = (f32[256,128]{1,0:T(8,128)}, f32[256,128]{1,0:T(8,128)}, f32[2]{0:T(128)}) custom-call(f32[256,128]{1,0:T(8,128)S(1)} %get-tuple-element.9.rewards, f32[32,8,128]{2,1,0:T(8,128)S(1)} %get-tuple-element.10.s_buf, f32[32,8,128]{2,1,0:T(8,128)S(1)} %get-tuple-element.11.p_buf, f32[8,128]{1,0:T(8,128)S(1)} %get-tuple-element.12.carry_ref, ...), custom_call_target="tpu_custom_call" | custom-call | tf_op jit(solution)/shard_map/pallas_call | solution.py:180
where the time goes:
time: 14.4 us; the launch traced here: 14.2 us
  Pallas kernels  12.3 us (85%)
  between operations  1.93 us (13%)
    pallas_call x1, Pallas kernels, local(): pl.pallas_call(functools.partial(kernel, T, E), out_shape=(pltpu.VMEM(blo...  11.3 us
    pallas_call x1, Pallas kernels, local(): pl.pallas_call(functools.partial(finish, T, E), out_shape=(jax.ShapeDtype...  0.95 us

commit v1 on v0

v1 whole, which is shorter than its diff:
```python
import functools

import jax
import jax.numpy as jnp
from jax import lax
from jax.experimental import pallas as pl
from jax.experimental.pallas import tpu as pltpu
from jax.sharding import PartitionSpec as P

SUB = 8
ROWS = 8
PARTS = 2


def compose_rows(summed, product, row):
    step = 1
    while step < SUB:
        inside = row < SUB - step
        later_sum = jnp.where(inside, pltpu.roll(summed, SUB - step, 0), 0.0)
        later_product = jnp.where(inside, pltpu.roll(product, SUB - step, 0), 1.0)
        summed = summed + product * later_sum
        product = product * later_product
        step *= 2
    return summed, product


def kernel(T, E, rewards_hbm, dones_hbm, horizon_hbm, bootstrap_hbm, prior,
           rewards, s_buf, p_buf, carry_ref, ebuf, prior_ref,
           dones, horizon_ref, bootstrap_ref, tbuf, xbuf,
           load_sem, small_sem, send_sem, recv_sem):
    t = lax.axis_index("tm")
    e = lax.axis_index("env")
    me = t * E + e
    peers = [k + jnp.where(k >= me, 1, 0) for k in range(T * E - 1)]
    loads = [pltpu.make_async_copy(rewards_hbm, rewards, load_sem.at[0]),
             pltpu.make_async_copy(dones_hbm, dones, load_sem.at[1])]
    smalls = [pltpu.make_async_copy(horizon_hbm, horizon_ref, small_sem.at[0]),
              pltpu.make_async_copy(bootstrap_hbm, bootstrap_ref, small_sem.at[1])]
    for load in smalls[:1] + loads + smalls[1:]:
        load.start()
    barrier = pltpu.get_barrier_semaphore()
    for peer in peers:
        pl.semaphore_signal(barrier, inc=1, device_id=peer, device_id_type=pl.DeviceIdType.LOGICAL)
    rows, lanes = rewards.shape
    chunk = rows // SUB
    shape = (SUB, lanes)
    row = lax.broadcasted_iota(jnp.int32, shape, 0)
    smalls[0].wait()
    discount = jnp.broadcast_to(1.0 - 1.0 / horizon_ref[...], shape)
    for load in loads:
        load.wait()
    s = jnp.zeros(shape, jnp.float32)
    p = jnp.ones(shape, jnp.float32)
    zero = jnp.zeros(shape, jnp.float32)
    s1, p1, s2, sp, p2 = zero, zero, zero, zero, zero
    for k in reversed(range(chunk)):
        r = rewards[pl.ds(k, SUB, stride=chunk), :]
        f = jnp.where(dones[pl.ds(k, SUB, stride=chunk), :] == 0, discount, 0.0)
        s = r + f * s
        p = f * p
        s_buf[k] = s
        p_buf[k] = p
        s1 = s1 + s
        p1 = p1 + p
        s2 = s2 + s * s
        sp = sp + s * p
        p2 = p2 + p * p
    full_s, full_p = compose_rows(s, p, row)
    last = row == SUB - 1
    a = jnp.where(last, 0.0, pltpu.roll(full_s, SUB - 1, 0))
    b = jnp.where(last, 1.0, pltpu.roll(full_p, SUB - 1, 0))
    down = lambda value: jnp.sum(value, axis=0, keepdims=True)
    smalls[1].wait()
    known = jnp.where(t == T - 1, bootstrap_ref[...], jnp.zeros((1, lanes), jnp.float32))
    a = a + b * known
    rest = sp + a * p2
    tbuf[me, 0:1] = full_s[0:1] + full_p[0:1] * known
    tbuf[me, 1:2] = full_p[0:1]
    tbuf[me, 2:3] = down(s1 + p1 * a)
    tbuf[me, 3:4] = down(p1 * b)
    tbuf[me, 4:5] = down(s2 + a * (sp + rest))
    tbuf[me, 5:6] = down(2.0 * b * rest)
    tbuf[me, 6:7] = down(b * b * p2)
    tbuf[me, 7:8] = prior[...]
    pl.semaphore_wait(barrier, T * E - 1)
    for peer in peers:
        pltpu.make_async_remote_copy(
            tbuf.at[me], tbuf.at[me], send_sem, recv_sem,
            device_id=peer, device_id_type=pl.DeviceIdType.LOGICAL).start()
    every = tbuf.at[0:T * E - 1]
    pltpu.make_async_copy(every, every, recv_sem).wait()
    x = jnp.zeros((E, lanes), jnp.float32)
    first = jnp.zeros((E, lanes), jnp.float32)
    second = jnp.zeros((E, lanes), jnp.float32)
    for j in reversed(range(T)):
        xbuf[j] = x
        part = pl.ds(j * E, E)
        first = first + tbuf[part, 2] + tbuf[part, 3] * x
        second = second + tbuf[part, 4] + x * (tbuf[part, 5] + x * tbuf[part, 6])
        x = tbuf[part, 0] + tbuf[part, 1] * x
    mine = xbuf[t, pl.ds(e, 1), :]
    prior_ref[...] = tbuf[0, 7:8]
    ebuf[0] = first
    ebuf[1] = second
    carry_ref[...] = a + b * mine
    pltpu.make_async_copy(every, every, send_sem).wait()


def pair_priors(mean, var, out):
    lane = lax.broadcasted_iota(jnp.int32, out.shape, 1)
    out[...] = jnp.where(lane == 0, mean[0], jnp.where(lane == out.shape[1] // 2, var[0], 0.0))


def finish(T, E, rewards, s_buf, p_buf, carry_ref, ebuf, prior_ref, out_rewards, out_returns, out_stats,
           rewards_out, returns_out, stats, sems):
    rows, lanes = rewards.shape
    chunk = rows // SUB
    entries = float(rows * T * lanes * E)
    prior_count = entries
    merged = prior_count + entries
    prior = prior_ref[...]
    is_mean = lax.broadcasted_iota(jnp.int32, prior.shape, 1) < lanes // 2
    first = jnp.sum(ebuf[0], axis=0, keepdims=True) * (1.0 / entries)
    second = jnp.sum(ebuf[1], axis=0, keepdims=True) * (1.0 / merged)
    across = lambda value: jnp.sum(value, axis=1, keepdims=True)
    average = across(first)
    delta = across(first - jnp.where(is_mean, prior, 0.0))
    squares = across(second + jnp.where(is_mean, 0.0, prior * (prior_count / merged)))
    new_mean = average - delta * (prior_count / merged)
    variance = (squares - average * average * (entries / merged)
                + delta * delta * (prior_count / merged * (entries / merged)))
    inverse = jnp.broadcast_to(lax.rsqrt(variance + 1e-08), (SUB, lanes))
    copies = []

    def send(source, target, rank):
        copy = pltpu.make_async_copy(source, target, sems.at[rank])
        copy.start()
        copies.append(copy)

    y = carry_ref[...] * inverse
    for k in range(chunk):
        returns_out[pl.ds(k, SUB, stride=chunk), :] = s_buf[k] * inverse + p_buf[k] * y
    send(returns_out, out_returns, 0)
    part = rows // PARTS
    for i in range(PARTS):
        for k in range(i * part, (i + 1) * part, SUB):
            rewards_out[k:k + SUB] = rewards[k:k + SUB] * inverse
        where = pl.ds(i * part, part)
        send(rewards_out.at[where], out_rewards.at[where], 2 + i)
    stats[0] = new_mean[0, 0]
    stats[1] = variance[0, 0]
    send(stats, out_stats, 1)
    for copy in copies:
        copy.wait()


def local(T, E, rewards, dones, horizon, bootstrap, prior_mean, prior_var):
    rows, lanes = rewards.shape
    block = (rows, lanes)
    vmem = pl.BlockSpec(memory_space=pltpu.VMEM)
    hbm = pl.BlockSpec(memory_space=pltpu.HBM)
    shapes = (block, (rows // SUB, SUB, lanes), (rows // SUB, SUB, lanes), (SUB, lanes), (2, E, lanes), (1, lanes))
    exchange = pl.pallas_call(
        functools.partial(kernel, T, E),
        out_shape=tuple(pltpu.VMEM(shape, jnp.float32) for shape in shapes),
        in_specs=[hbm] * 4 + [vmem],
        out_specs=(vmem,) * 6,
        scratch_shapes=[
            pltpu.VMEM(block, jnp.int32),
            pltpu.VMEM((1, lanes), jnp.float32),
            pltpu.VMEM((1, lanes), jnp.float32),
            pltpu.VMEM((T * E, ROWS, lanes), jnp.float32),
            pltpu.VMEM((T, E, lanes), jnp.float32),
            pltpu.SemaphoreType.DMA((2,)),
            pltpu.SemaphoreType.DMA((2,)),
            pltpu.SemaphoreType.DMA,
            pltpu.SemaphoreType.DMA,
        ],
        compiler_params=pltpu.CompilerParams(collective_id=0, has_side_effects=True),
    )
    smem = pl.BlockSpec(memory_space=pltpu.SMEM)
    pair = pl.pallas_call(
        pair_priors, out_shape=jax.ShapeDtypeStruct((1, lanes), jnp.float32),
        in_specs=[smem] * 2, out_specs=vmem)
    prior = lax.cond(lax.axis_index("tm") + lax.axis_index("env") == 0, pair,
                     lambda *_: jnp.zeros((1, lanes), jnp.float32), prior_mean, prior_var)
    between = exchange(rewards, dones, horizon.reshape(1, lanes), bootstrap.reshape(1, lanes), prior)
    return pl.pallas_call(
        functools.partial(finish, T, E),
        out_shape=(jax.ShapeDtypeStruct(block, jnp.float32),
                   jax.ShapeDtypeStruct(block, jnp.float32),
                   jax.ShapeDtypeStruct((2,), jnp.float32)),
        in_specs=[vmem] * 6,
        out_specs=(hbm, hbm, hbm),
        scratch_shapes=[
            pltpu.VMEM(block, jnp.float32),
            pltpu.VMEM(block, jnp.float32),
            pltpu.SMEM((2,), jnp.float32),
            pltpu.SemaphoreType.DMA((2 + PARTS,)),
        ],
        compiler_params=pltpu.CompilerParams(vmem_limit_bytes=4 * 2**20),
    )(*between)


def solution(mesh):
    T, E = mesh.shape["tm"], mesh.shape["env"]
    return jax.shard_map(
        functools.partial(local, T, E),
        mesh=mesh,
        in_specs=(P("tm", "env"), P("tm", "env"), P("env"), P("env"), P(), P()),
        out_specs=(P("tm", "env"), P("tm", "env"), P()),
        check_vma=False,
    )
```

time: 14.4 us -> 11.8 us (0.82)
  Pallas kernels: 12.3 us -> 11 us
  between operations: 1.93 us -> 0.65 us
    pallas_call x1 -> x2, Pallas kernels: 11.3 us -> 10 us  [the longest x1 8.75 us: local(): exchange(rewards, dones, horizon.reshape(1, lanes), bootstrap.reshape(1,...]
where the time goes in v1:
time: 11.8 us; the launch traced here: 11.6 us
  Pallas kernels  11 us (93%)
  between operations  0.65 us (6%)
    pallas_call x1, Pallas kernels, local(): exchange(rewards, dones, horizon.reshape(1, lanes), bootstrap.reshape(1,...  8.75 us
    pallas_call x1, Pallas kernels, local(): lax.cond(lax.axis_index('tm') + lax.axis_index('env') == 0, pair, lambda...  1.3 us
    pallas_call x1, Pallas kernels, local(): pl.pallas_call(functools.partial(finish, T, E), out_shape=(jax.ShapeDtype...  0.92 us

profile of v1, /device:TPU:0, one launch (start us, length us, event | category | flops | bytes accessed | tf_op | source)
XLA Modules:
  0.0 11.6 jit_solution(12235535352460438737)
XLA Ops:
  0.6 1.3 %conditional.1 = (f32[1,128]{1,0:T(1,128)S(1)}) conditional(s32[]{:T(128)} %convert_element_type.3, () %tuple.13, (f32[1]{0:T(128)}, f32[1]{0:T(128)}) %tuple.14), branch_computations={%region_0.0_spmd, %region_1.0_spmd} | conditional | bytes 524 | solution.py:185
  0.7 1.3 %branch_1_fun.1 = f32[1,128]{1,0:T(1,128)S(1)} custom-call(f32[1]{0:T(128)} %get-tuple-element.26.mean, f32[1]{0:T(128)} %get-tuple-element.27.var), custom_call_target="tpu_custom_call" | custom-call | tf_op jit(solution)/shard_map/cond/branch_1_fun/pallas_call | solution.py:185
  2.0 8.7 %shard_map.87 = (f32[256,128]{1,0:T(8,128)S(1)}, f32[32,8,128]{2,1,0:T(8,128)S(1)}, f32[32,8,128]{2,1,0:T(8,128)S(1)}, f32[8,128]{1,0:T(8,128)S(1)}, f32[2,8,128]{2,1,0:T(8,128)S(1)}, /*index=5*/f32[1,128]{1,0:T(1,128)S(1)}) custom-call(f32[256,128]{1,0:T(8,128)} %rewards_hbm.1, s32[256,128]{1,0:T(8,128)} %dones_hbm.1, f32[1,128]{1,0:T(1,128)} %bitcast.2, ...), custom_call_target="tpu_custom_call" | custom-call | tf_op jit(solution)/shard_map/pallas_call | solution.py:187
  10.7 0.9 %shard_map.88 = (f32[256,128]{1,0:T(8,128)}, f32[256,128]{1,0:T(8,128)}, f32[2]{0:T(128)}) custom-call(f32[256,128]{1,0:T(8,128)S(1)} %get-tuple-element.18.rewards, f32[32,8,128]{2,1,0:T(8,128)S(1)} %get-tuple-element.19.s_buf, f32[32,8,128]{2,1,0:T(8,128)S(1)} %get-tuple-element.20.p_buf, f32[8,128]{1,0:T(8,128)S(1)} %get-tuple-element.21.carry_ref, ...), custom_call_target="tpu_custom_call" | custom-call | tf_op jit(solution)/shard_map/pallas_call | solution.py:188

commit v2 on v1

v2 whole, which is shorter than its diff:
```python
import functools

import jax
import jax.numpy as jnp
from jax import lax
from jax.experimental import pallas as pl
from jax.experimental.pallas import tpu as pltpu
from jax.sharding import PartitionSpec as P

SUB = 8
ROWS = 8


def compose_rows(summed, product, row):
    step = 1
    while step < SUB:
        inside = row < SUB - step
        later_sum = jnp.where(inside, pltpu.roll(summed, SUB - step, 0), 0.0)
        later_product = jnp.where(inside, pltpu.roll(product, SUB - step, 0), 1.0)
        summed = summed + product * later_sum
        product = product * later_product
        step *= 2
    return summed, product


def kernel(T, E, rewards_hbm, dones_hbm, horizon_hbm, bootstrap_hbm, prior,
           rewards, s_buf, p_buf, carry_ref, ebuf, prior_ref,
           dones, horizon_ref, bootstrap_ref, tbuf, xbuf, measure,
           load_sem, small_sem, send_sem, recv_sem):
    t = lax.axis_index("tm")
    e = lax.axis_index("env")
    me = t * E + e
    peers = [k + jnp.where(k >= me, 1, 0) for k in range(T * E - 1)]
    pieces = [pltpu.make_async_copy(source.at[i], target.at[:, i], load_sem.at[j])
              for j, (source, target) in enumerate(((rewards_hbm, rewards), (dones_hbm, dones)))
              for i in range(SUB)]
    loads = [pltpu.make_async_copy(target, target, load_sem.at[j]) for j, target in enumerate((rewards, dones))]
    smalls = [pltpu.make_async_copy(horizon_hbm, horizon_ref, small_sem.at[0]),
              pltpu.make_async_copy(bootstrap_hbm, bootstrap_ref, small_sem.at[1])]
    for load in smalls[:1] + pieces + smalls[1:]:
        load.start()
    barrier = pltpu.get_barrier_semaphore()
    for peer in reversed(peers):
        pl.semaphore_signal(barrier, inc=1, device_id=peer, device_id_type=pl.DeviceIdType.LOGICAL)
    chunk, _, lanes = rewards.shape
    shape = (SUB, lanes)
    row = lax.broadcasted_iota(jnp.int32, shape, 0)
    smalls[0].wait()
    discount = jnp.broadcast_to(1.0 - 1.0 / horizon_ref[...], shape)
    for load in loads:
        load.wait()
    s = jnp.zeros(shape, jnp.float32)
    p = jnp.ones(shape, jnp.float32)
    zero = jnp.zeros(shape, jnp.float32)
    s1, p1, s2, sp, p2 = zero, zero, zero, zero, zero
    for k in reversed(range(chunk)):
        r = rewards[k]
        f = jnp.where(dones[k] == 0, discount, 0.0)
        s = r + f * s
        p = f * p
        s_buf[k] = s
        p_buf[k] = p
        s1 = s1 + s
        p1 = p1 + p
        s2 = s2 + s * s
        sp = sp + s * p
        p2 = p2 + p * p
    full_s, full_p = compose_rows(s, p, row)
    last = row == SUB - 1
    a = jnp.where(last, 0.0, pltpu.roll(full_s, SUB - 1, 0))
    b = jnp.where(last, 1.0, pltpu.roll(full_p, SUB - 1, 0))
    down = lambda value: jnp.sum(value, axis=0, keepdims=True)
    smalls[1].wait()
    known = jnp.where(t == T - 1, bootstrap_ref[...], jnp.zeros((1, lanes), jnp.float32))
    a = a + b * known
    rest = sp + a * p2
    fold = lambda value: value + pltpu.roll(value, lanes // 2, 1)
    half = lax.broadcasted_iota(jnp.int32, (1, lanes), 1) < lanes // 2
    leading = full_s[0:1] + full_p[0:1] * known
    tbuf[me, 0:1] = jnp.where(half, fold(down(s1 + p1 * a)), fold(down(s2 + a * (sp + rest))))

    @pl.when(t == T - 1)
    def _():
        tbuf[me, 1:2] = leading

    @pl.when(t < T - 1)
    def _():
        tbuf[me, 1:2] = down(p1 * b)
        tbuf[me, 2:3] = down(2.0 * b * rest)
        tbuf[me, 3:4] = down(b * b * p2)
        tbuf[me, 4:5] = leading
        tbuf[me, 5:6] = full_p[0:1]
        tbuf[me, 6:7] = prior[...]

    pl.semaphore_wait(barrier, T * E - 1)
    total = E * sum(rows_sent(T, j) for j in range(T))
    for count in sorted({rows_sent(T, j) for j in range(T)}):
        blocks = [j for j in range(T) if rows_sent(T, j) == count]

        @pl.when(jnp.logical_and(t >= blocks[0], t <= blocks[-1]))
        def _():
            for peer in peers:
                pltpu.make_async_remote_copy(
                    tbuf.at[me, 0:count], tbuf.at[me, 0:count], send_sem, recv_sem,
                    device_id=peer, device_id_type=pl.DeviceIdType.LOGICAL).start()
            arrived = measure.at[0:total - count]
            pltpu.make_async_copy(arrived, arrived, recv_sem).wait()
            left = measure.at[0:(T * E - 1) * count]
            pltpu.make_async_copy(left, left, send_sem).wait()

    packed = jnp.zeros((E, lanes), jnp.float32)
    first = jnp.zeros((E, lanes), jnp.float32)
    second = jnp.zeros((E, lanes), jnp.float32)
    x = jnp.zeros((E, lanes), jnp.float32)
    for j in reversed(range(T)):
        part = pl.ds(j * E, E)
        xbuf[j] = x
        packed = packed + tbuf[part, 0]
        if j == T - 1:
            x = tbuf[part, 1]
            continue
        first = first + tbuf[part, 1] * x
        second = second + x * (tbuf[part, 2] + x * tbuf[part, 3])
        if j:
            x = tbuf[part, 4] + tbuf[part, 5] * x
    mine = xbuf[t, pl.ds(e, 1), :]
    prior_ref[0:1] = tbuf[reader(T, E), 6:7]
    prior_ref[1:2] = tbuf[reader(T, E) + 1, 6:7]
    ebuf[0] = packed
    ebuf[1] = first
    ebuf[2] = second
    carry_ref[...] = a + b * mine


def rows_sent(T, block):
    if block >= T - 2:
        return 2 if block == T - 1 else 7
    return 6 if block else 4


def reader(T, E):
    return max((T - 1) * E - 2, 0)


def pick(value, out):
    lane = lax.broadcasted_iota(jnp.int32, out.shape, 1)
    out[...] = jnp.where(lane == 0, value[0], 0.0)


def finish(T, E, rewards, s_buf, p_buf, carry_ref, ebuf, prior_ref, out_rewards, out_returns, out_stats,
           rewards_out, returns_out, stats, sems):
    chunk, _, lanes = rewards.shape
    entries = float(chunk * SUB * T * lanes * E)
    prior_count = entries
    half = lax.broadcasted_iota(jnp.int32, (1, lanes), 1) < lanes // 2
    merged = prior_count + entries
    down = lambda value: jnp.sum(value, axis=0, keepdims=True)
    packed = down(ebuf[0])
    first = (down(ebuf[1]) + jnp.where(half, packed, 0.0)) * (1.0 / entries)
    second = (down(ebuf[2]) + jnp.where(half, 0.0, packed)) * (1.0 / merged)
    across = lambda value: jnp.sum(value, axis=1, keepdims=True)
    average = across(first)
    delta = across(first - prior_ref[0:1])
    squares = across(second + prior_ref[1:2] * (prior_count / merged))
    new_mean = average - delta * (prior_count / merged)
    variance = (squares - average * average * (entries / merged)
                + delta * delta * (prior_count / merged * (entries / merged)))
    inverse = jnp.broadcast_to(lax.rsqrt(variance + 1e-08), (SUB, lanes))

    def send(source, target, rank):
        for i in range(SUB):
            pltpu.make_async_copy(source.at[:, i], target.at[i], sems.at[rank]).start()

    y = carry_ref[...] * inverse
    for k in range(chunk):
        returns_out[k] = s_buf[k] * inverse + p_buf[k] * y
    send(returns_out, out_returns, 0)
    for k in range(chunk):
        rewards_out[k] = rewards[k] * inverse
    send(rewards_out, out_rewards, 1)
    stats[0] = new_mean[0, 0]
    stats[1] = variance[0, 0]
    last = pltpu.make_async_copy(stats, out_stats, sems.at[2])
    last.start()
    pltpu.make_async_copy(returns_out, returns_out, sems.at[0]).wait()
    pltpu.make_async_copy(rewards_out, rewards_out, sems.at[1]).wait()
    last.wait()


def local(T, E, rewards, dones, horizon, bootstrap, prior_mean, prior_var):
    rows, lanes = rewards.shape
    split = (SUB, rows // SUB, lanes)
    vmem = pl.BlockSpec(memory_space=pltpu.VMEM)
    hbm = pl.BlockSpec(memory_space=pltpu.HBM)
    steps = (rows // SUB, SUB, lanes)
    shapes = (steps, steps, steps, (SUB, lanes), (3, E, lanes), (2, lanes))
    exchange = pl.pallas_call(
        functools.partial(kernel, T, E),
        out_shape=tuple(pltpu.VMEM(shape, jnp.float32) for shape in shapes),
        in_specs=[hbm] * 4 + [vmem],
        out_specs=(vmem,) * 6,
        scratch_shapes=[
            pltpu.VMEM(steps, jnp.int32),
            pltpu.VMEM((1, lanes), jnp.float32),
            pltpu.VMEM((1, lanes), jnp.float32),
            pltpu.VMEM((T * E, ROWS, lanes), jnp.float32),
            pltpu.VMEM((T, E, lanes), jnp.float32),
            pltpu.VMEM((T * E * ROWS, lanes), jnp.float32),
            pltpu.SemaphoreType.DMA((2,)),
            pltpu.SemaphoreType.DMA((2,)),
            pltpu.SemaphoreType.DMA,
            pltpu.SemaphoreType.DMA,
        ],
        compiler_params=pltpu.CompilerParams(collective_id=0, has_side_effects=True),
    )
    smem = pl.BlockSpec(memory_space=pltpu.SMEM)
    alone = pl.pallas_call(
        pick, out_shape=jax.ShapeDtypeStruct((1, lanes), jnp.float32), in_specs=[smem], out_specs=vmem)
    me = lax.axis_index("tm") * E + lax.axis_index("env")
    prior = lax.switch(
        jnp.clip(me - reader(T, E) + 1, 0, 3),
        (lambda *_: jnp.zeros((1, lanes), jnp.float32), lambda mean, _: alone(mean), lambda _, var: alone(var),
         lambda *_: jnp.zeros((1, lanes), jnp.float32)), prior_mean, prior_var)
    between = exchange(rewards.reshape(split), dones.reshape(split), horizon.reshape(1, lanes), bootstrap.reshape(1, lanes), prior)
    scaled_rewards, scaled_returns, stats = pl.pallas_call(
        functools.partial(finish, T, E),
        out_shape=(jax.ShapeDtypeStruct(split, jnp.float32),
                   jax.ShapeDtypeStruct(split, jnp.float32),
                   jax.ShapeDtypeStruct((2,), jnp.float32)),
        in_specs=[vmem] * 6,
        out_specs=(hbm, hbm, hbm),
        scratch_shapes=[
            pltpu.VMEM(steps, jnp.float32),
            pltpu.VMEM(steps, jnp.float32),
            pltpu.SMEM((2,), jnp.float32),
            pltpu.SemaphoreType.DMA((3,)),
        ],
        compiler_params=pltpu.CompilerParams(vmem_limit_bytes=4 * 2**20),
    )(*between)
    return scaled_rewards.reshape(rows, lanes), scaled_returns.reshape(rows, lanes), stats


def solution(mesh):
    T, E = mesh.shape["tm"], mesh.shape["env"]
    return jax.shard_map(
        functools.partial(local, T, E),
        mesh=mesh,
        in_specs=(P("tm", "env"), P("tm", "env"), P("env"), P("env"), P(), P()),
        out_specs=(P("tm", "env"), P("tm", "env"), P()),
        check_vma=False,
    )
```

time: 11.8 us -> 11.5 us (0.975)
  Pallas kernels: 11 us -> 10.6 us
    pallas_call x2 -> x1, Pallas kernels: 10 us -> 9.81 us  [local(): exchange(rewards.reshape(split), dones.reshape(split), horizon.reshape(1,...]
where the time goes in v2:
time: 11.5 us; the launch traced here: 11.3 us
  Pallas kernels  10.6 us (92%)
  between operations  0.66 us (6%)
    pallas_call x1, Pallas kernels, local(): exchange(rewards.reshape(split), dones.reshape(split), horizon.reshape(1,...  9.81 us
    pallas_call x1, Pallas kernels, local(): pl.pallas_call(functools.partial(finish, T, E), out_shape=(jax.ShapeDtype...  0.84 us

profile of v2, /device:TPU:0, one launch (start us, length us, event | category | flops | bytes accessed | tf_op | source)
XLA Modules:
  0.0 11.3 jit_solution(18207472415789181569)
XLA Ops:
  0.7 9.8 %shard_map.93 = (f32[32,8,128]{2,1,0:T(8,128)S(1)}, f32[32,8,128]{2,1,0:T(8,128)S(1)}, f32[32,8,128]{2,1,0:T(8,128)S(1)}, f32[8,128]{1,0:T(8,128)S(1)}, f32[3,8,128]{2,1,0:T(8,128)S(1)}, /*index=5*/f32[2,128]{1,0:T(2,128)S(1)}) custom-call(f32[8,32,128]{2,1,0:T(8,128)} %bitcast.6, s32[8,32,128]{2,1,0:T(8,128)} %bitcast.7, f32[1,128]{1,0:T(1,128)} %bitcast.8, ...), custom_call_target="tpu_custom_call" | custom-call | tf_op jit(solution)/shard_map/pallas_call | solution.py:224
  10.5 0.8 %shard_map.94 = (f32[8,32,128]{2,1,0:T(8,128)}, f32[8,32,128]{2,1,0:T(8,128)}, f32[2]{0:T(128)}) custom-call(f32[32,8,128]{2,1,0:T(8,128)S(1)} %get-tuple-element.19.rewards, f32[32,8,128]{2,1,0:T(8,128)S(1)} %get-tuple-element.20.s_buf, f32[32,8,128]{2,1,0:T(8,128)S(1)} %get-tuple-element.21.p_buf, f32[8,128]{1,0:T(8,128)S(1)} %get-tuple-element.22.carry_ref, ...), custom_call_target="tpu_custom_call" | custom-call | tf_op jit(solution)/shard_map/pallas_call | solution.py:225
  (2 shorter events, 0.0 us)

commit v3 on v2

--- a/solution.py
+++ b/solution.py
@@ -26,29 +26,28 @@
 def kernel(T, E, rewards_hbm, dones_hbm, horizon_hbm, bootstrap_hbm, prior,
            rewards, s_buf, p_buf, carry_ref, ebuf, prior_ref,
            dones, horizon_ref, bootstrap_ref, tbuf, xbuf, measure,
-           load_sem, small_sem, send_sem, recv_sem):
+           load_sem, send_sem, recv_sem):
     t = lax.axis_index("tm")
     e = lax.axis_index("env")
     me = t * E + e
     peers = [k + jnp.where(k >= me, 1, 0) for k in range(T * E - 1)]
-    pieces = [pltpu.make_async_copy(source.at[i], target.at[:, i], load_sem.at[j])
-              for j, (source, target) in enumerate(((rewards_hbm, rewards), (dones_hbm, dones)))
-              for i in range(SUB)]
-    loads = [pltpu.make_async_copy(target, target, load_sem.at[j]) for j, target in enumerate((rewards, dones))]
-    smalls = [pltpu.make_async_copy(horizon_hbm, horizon_ref, small_sem.at[0]),
-              pltpu.make_async_copy(bootstrap_hbm, bootstrap_ref, small_sem.at[1])]
-    for load in smalls[:1] + pieces + smalls[1:]:
-        load.start()
+    chunk, _, lanes = rewards.shape
+    pltpu.make_async_copy(horizon_hbm, horizon_ref, load_sem).start()
+    pltpu.make_async_copy(bootstrap_hbm, bootstrap_ref, load_sem).start()
+    for source, target in ((rewards_hbm, rewards), (dones_hbm, dones)):
+        for i in range(SUB):
+            pltpu.make_async_copy(source.at[i], target.at[:, i], load_sem).start()
     barrier = pltpu.get_barrier_semaphore()
-    for peer in reversed(peers):
+    def greet(peer):
         pl.semaphore_signal(barrier, inc=1, device_id=peer, device_id_type=pl.DeviceIdType.LOGICAL)
-    chunk, _, lanes = rewards.shape
+
+    lax.fori_loop(0, T * E - 1 - me, lambda i, _: greet(T * E - 1 - i), None)
+    lax.fori_loop(0, me, lambda i, _: greet(me - 1 - i), None)
     shape = (SUB, lanes)
     row = lax.broadcasted_iota(jnp.int32, shape, 0)
-    smalls[0].wait()
+    loaded = measure.at[0:2 * chunk * SUB + 2]
+    pltpu.make_async_copy(loaded, loaded, load_sem).wait()
     discount = jnp.broadcast_to(1.0 - 1.0 / horizon_ref[...], shape)
-    for load in loads:
-        load.wait()
     s = jnp.zeros(shape, jnp.float32)
     p = jnp.ones(shape, jnp.float32)
     zero = jnp.zeros(shape, jnp.float32)
@@ -70,7 +69,6 @@
     a = jnp.where(last, 0.0, pltpu.roll(full_s, SUB - 1, 0))
     b = jnp.where(last, 1.0, pltpu.roll(full_p, SUB - 1, 0))
     down = lambda value: jnp.sum(value, axis=0, keepdims=True)
-    smalls[1].wait()
     known = jnp.where(t == T - 1, bootstrap_ref[...], jnp.zeros((1, lanes), jnp.float32))
     a = a + b * known
     rest = sp + a * p2
@@ -88,9 +86,8 @@
         tbuf[me, 1:2] = down(p1 * b)
         tbuf[me, 2:3] = down(2.0 * b * rest)
         tbuf[me, 3:4] = down(b * b * p2)
-        tbuf[me, 4:5] = leading
+        tbuf[me, 4:5] = jnp.where(t == 0, prior[...], leading)
         tbuf[me, 5:6] = full_p[0:1]
-        tbuf[me, 6:7] = prior[...]
 
     pl.semaphore_wait(barrier, T * E - 1)
     total = E * sum(rows_sent(T, j) for j in range(T))
@@ -99,10 +96,13 @@
 
         @pl.when(jnp.logical_and(t >= blocks[0], t <= blocks[-1]))
         def _():
-            for peer in peers:
+            def give(peer, _):
                 pltpu.make_async_remote_copy(
                     tbuf.at[me, 0:count], tbuf.at[me, 0:count], send_sem, recv_sem,
                     device_id=peer, device_id_type=pl.DeviceIdType.LOGICAL).start()
+
+            lax.fori_loop(0, me, give, None)
+            lax.fori_loop(me + 1, T * E, give, None)
             arrived = measure.at[0:total - count]
             pltpu.make_async_copy(arrived, arrived, recv_sem).wait()
             left = measure.at[0:(T * E - 1) * count]
@@ -124,8 +124,8 @@
         if j:
             x = tbuf[part, 4] + tbuf[part, 5] * x
     mine = xbuf[t, pl.ds(e, 1), :]
-    prior_ref[0:1] = tbuf[reader(T, E), 6:7]
-    prior_ref[1:2] = tbuf[reader(T, E) + 1, 6:7]
+    prior_ref[0:1] = tbuf[reader(T, E), 4:5]
+    prior_ref[1:2] = tbuf[reader(T, E) + 1, 4:5]
     ebuf[0] = packed
     ebuf[1] = first
     ebuf[2] = second
@@ -133,13 +133,13 @@
 
 
 def rows_sent(T, block):
-    if block >= T - 2:
-        return 2 if block == T - 1 else 7
-    return 6 if block else 4
+    if block == T - 1:
+        return 2
+    return 6 if block else 5
 
 
 def reader(T, E):
-    return max((T - 1) * E - 2, 0)
+    return 0
 
 
 def pick(value, out):
@@ -205,9 +205,8 @@
             pltpu.VMEM((1, lanes), jnp.float32),
             pltpu.VMEM((T * E, ROWS, lanes), jnp.float32),
             pltpu.VMEM((T, E, lanes), jnp.float32),
-            pltpu.VMEM((T * E * ROWS, lanes), jnp.float32),
-            pltpu.SemaphoreType.DMA((2,)),
-            pltpu.SemaphoreType.DMA((2,)),
+            pltpu.VMEM((max(T * E * ROWS, 2 * rows + 2), lanes), jnp.float32),
+            pltpu.SemaphoreType.DMA,
             pltpu.SemaphoreType.DMA,
             pltpu.SemaphoreType.DMA,
         ],

time: 11.5 us -> 11.4 us (level)
    pallas_call x1, Pallas kernels: 9.81 us -> 9.02 us  [local(): exchange(rewards.reshape(split), dones.reshape(split), horizon.reshape(1,...]
    pallas_call x0 -> x1, Pallas kernels: none -> 0.65 us  [local(): alone(mean)]
where the time goes in v3:
time: 11.4 us; the launch traced here: 11.2 us
  Pallas kernels  10.5 us (92%)
  between operations  0.66 us (6%)
    pallas_call x1, Pallas kernels, local(): exchange(rewards.reshape(split), dones.reshape(split), horizon.reshape(1,...  9.02 us
    pallas_call x1, Pallas kernels, local(): pl.pallas_call(functools.partial(finish, T, E), out_shape=(jax.ShapeDtype...  0.84 us
    pallas_call x1, Pallas kernels, local(): alone(mean)  0.65 us

profile of v3, /device:TPU:0, one launch (start us, length us, event | category | flops | bytes accessed | tf_op | source)
XLA Modules:
  0.0 11.2 jit_solution(5063124727451905864)
XLA Ops:
  0.6 0.7 %conditional.1 = (f32[1,128]{1,0:T(1,128)S(1)}) conditional(s32[]{:T(128)} %clamp.3, () %tuple.20, (f32[1]{0:T(128)}) %tuple.23, (f32[1]{0:T(128)}) %tuple.24, () %tuple.21), branch_computations={%region_0.1_spmd, %region_1.2_spmd, %region_2.3_spmd, %region_3.4_... | conditional | bytes 524 | solution.py:219
  0.7 0.7 %branch_1_fun.1 = f32[1,128]{1,0:T(1,128)S(1)} custom-call(f32[1]{0:T(128)} %get-tuple-element.29.value), custom_call_target="tpu_custom_call" | custom-call | tf_op jit(solution)/shard_map/cond/branch_1_fun/pallas_call | solution.py:221
  1.3 9.0 %shard_map.93 = (f32[32,8,128]{2,1,0:T(8,128)S(1)}, f32[32,8,128]{2,1,0:T(8,128)S(1)}, f32[32,8,128]{2,1,0:T(8,128)S(1)}, f32[8,128]{1,0:T(8,128)S(1)}, f32[3,8,128]{2,1,0:T(8,128)S(1)}, /*index=5*/f32[2,128]{1,0:T(2,128)S(1)}) custom-call(f32[8,32,128]{2,1,0:T(8,128)} %bitcast.6, s32[8,32,128]{2,1,0:T(8,128)} %bitcast.7, f32[1,128]{1,0:T(1,128)} %bitcast.8, ...), custom_call_target="tpu_custom_call" | custom-call | tf_op jit(solution)/shard_map/pallas_call | solution.py:223
  10.4 0.8 %shard_map.94 = (f32[8,32,128]{2,1,0:T(8,128)}, f32[8,32,128]{2,1,0:T(8,128)}, f32[2]{0:T(128)}) custom-call(f32[32,8,128]{2,1,0:T(8,128)S(1)} %get-tuple-element.19.rewards, f32[32,8,128]{2,1,0:T(8,128)S(1)} %get-tuple-element.20.s_buf, f32[32,8,128]{2,1,0:T(8,128)S(1)} %get-tuple-element.21.p_buf, f32[8,128]{1,0:T(8,128)S(1)} %get-tuple-element.22.carry_ref, ...), custom_call_target="tpu_custom_call" | custom-call | tf_op jit(solution)/shard_map/pallas_call | solution.py:224

commit v4 on v3

--- a/solution.py
+++ b/solution.py
@@ -9,6 +9,7 @@
 
 SUB = 8
 ROWS = 8
+FIRST = 2
 
 
 def compose_rows(summed, product, row):
@@ -45,6 +46,10 @@
     lax.fori_loop(0, me, lambda i, _: greet(me - 1 - i), None)
     shape = (SUB, lanes)
     row = lax.broadcasted_iota(jnp.int32, shape, 0)
+    @pl.when(me < FIRST)
+    def _():
+        pl.semaphore_wait(barrier, T * E - 1)
+
     loaded = measure.at[0:2 * chunk * SUB + 2]
     pltpu.make_async_copy(loaded, loaded, load_sem).wait()
     discount = jnp.broadcast_to(1.0 - 1.0 / horizon_ref[...], shape)
@@ -89,7 +94,11 @@
         tbuf[me, 4:5] = jnp.where(t == 0, prior[...], leading)
         tbuf[me, 5:6] = full_p[0:1]
 
-    pl.semaphore_wait(barrier, T * E - 1)
+
+    @pl.when(me >= FIRST)
+    def _():
+        pl.semaphore_wait(barrier, T * E - 1)
+
     total = E * sum(rows_sent(T, j) for j in range(T))
     for count in sorted({rows_sent(T, j) for j in range(T)}):
         blocks = [j for j in range(T) if rows_sent(T, j) == count]

time: 11.4 us -> 11.3 us (level)
  no operation moved by 1% of the time
where the time goes in v4:
time: 11.3 us; the launch traced here: 11.2 us
  Pallas kernels  10.5 us (93%)
  between operations  0.66 us (6%)
    pallas_call x1, Pallas kernels, local(): exchange(rewards.reshape(split), dones.reshape(split), horizon.reshape(1,...  9.02 us
    pallas_call x1, Pallas kernels, local(): pl.pallas_call(functools.partial(finish, T, E), out_shape=(jax.ShapeDtype...  0.84 us
    pallas_call x1, Pallas kernels, local(): alone(mean)  0.65 us

profile of v4, /device:TPU:0, one launch (start us, length us, event | category | flops | bytes accessed | tf_op | source)
XLA Modules:
  0.0 11.2 jit_solution(3515576153920802877)
XLA Ops:
  0.6 0.7 %conditional.1 = (f32[1,128]{1,0:T(1,128)S(1)}) conditional(s32[]{:T(128)} %clamp.3, () %tuple.20, (f32[1]{0:T(128)}) %tuple.23, (f32[1]{0:T(128)}) %tuple.24, () %tuple.21), branch_computations={%region_0.1_spmd, %region_1.2_spmd, %region_2.3_spmd, %region_3.4_... | conditional | bytes 524 | solution.py:228
  0.7 0.7 %branch_1_fun.1 = f32[1,128]{1,0:T(1,128)S(1)} custom-call(f32[1]{0:T(128)} %get-tuple-element.29.value), custom_call_target="tpu_custom_call" | custom-call | tf_op jit(solution)/shard_map/cond/branch_1_fun/pallas_call | solution.py:230
  1.3 9.0 %shard_map.93 = (f32[32,8,128]{2,1,0:T(8,128)S(1)}, f32[32,8,128]{2,1,0:T(8,128)S(1)}, f32[32,8,128]{2,1,0:T(8,128)S(1)}, f32[8,128]{1,0:T(8,128)S(1)}, f32[3,8,128]{2,1,0:T(8,128)S(1)}, /*index=5*/f32[2,128]{1,0:T(2,128)S(1)}) custom-call(f32[8,32,128]{2,1,0:T(8,128)} %bitcast.6, s32[8,32,128]{2,1,0:T(8,128)} %bitcast.7, f32[1,128]{1,0:T(1,128)} %bitcast.8, ...), custom_call_target="tpu_custom_call" | custom-call | tf_op jit(solution)/shard_map/pallas_call | solution.py:232
  10.4 0.8 %shard_map.94 = (f32[8,32,128]{2,1,0:T(8,128)}, f32[8,32,128]{2,1,0:T(8,128)}, f32[2]{0:T(128)}) custom-call(f32[32,8,128]{2,1,0:T(8,128)S(1)} %get-tuple-element.19.rewards, f32[32,8,128]{2,1,0:T(8,128)S(1)} %get-tuple-element.20.s_buf, f32[32,8,128]{2,1,0:T(8,128)S(1)} %get-tuple-element.21.p_buf, f32[8,128]{1,0:T(8,128)S(1)} %get-tuple-element.22.carry_ref, ...), custom_call_target="tpu_custom_call" | custom-call | tf_op jit(solution)/shard_map/pallas_call | solution.py:233

commit v5 on v4

--- a/solution.py
+++ b/solution.py
@@ -42,8 +42,11 @@
     def greet(peer):
         pl.semaphore_signal(barrier, inc=1, device_id=peer, device_id_type=pl.DeviceIdType.LOGICAL)
 
-    lax.fori_loop(0, T * E - 1 - me, lambda i, _: greet(T * E - 1 - i), None)
-    lax.fori_loop(0, me, lambda i, _: greet(me - 1 - i), None)
+    late = 2 * t >= T
+    origin, turn = jnp.where(late, 0, T * E - 1), jnp.where(late, 1, -1)
+    before = jnp.where(late, me, T * E - 1 - me)
+    lax.fori_loop(0, before, lambda i, _: greet(origin + turn * i), None)
+    lax.fori_loop(before + 1, T * E, lambda i, _: greet(origin + turn * i), None)
     shape = (SUB, lanes)
     row = lax.broadcasted_iota(jnp.int32, shape, 0)
     @pl.when(me < FIRST)
@@ -77,17 +80,21 @@
     known = jnp.where(t == T - 1, bootstrap_ref[...], jnp.zeros((1, lanes), jnp.float32))
     a = a + b * known
     rest = sp + a * p2
-    fold = lambda value: value + pltpu.roll(value, lanes // 2, 1)
-    half = lax.broadcasted_iota(jnp.int32, (1, lanes), 1) < lanes // 2
     leading = full_s[0:1] + full_p[0:1] * known
-    tbuf[me, 0:1] = jnp.where(half, fold(down(s1 + p1 * a)), fold(down(s2 + a * (sp + rest))))
+    first = down(s1 + p1 * a)
+    second = down(s2 + a * (sp + rest))
 
     @pl.when(t == T - 1)
     def _():
-        tbuf[me, 1:2] = leading
+        tbuf[me, 0:1] = first
+        tbuf[me, 1:2] = second
+        tbuf[me, 2:3] = leading
 
     @pl.when(t < T - 1)
     def _():
+        fold = lambda value: value + pltpu.roll(value, lanes // 2, 1)
+        half = lax.broadcasted_iota(jnp.int32, (1, lanes), 1) < lanes // 2
+        tbuf[me, 0:1] = jnp.where(half, fold(first), fold(second))
         tbuf[me, 1:2] = down(p1 * b)
         tbuf[me, 2:3] = down(2.0 * b * rest)
         tbuf[me, 3:4] = down(b * b * p2)
@@ -124,10 +131,12 @@
     for j in reversed(range(T)):
         part = pl.ds(j * E, E)
         xbuf[j] = x
+        if j == T - 1:
+            first = first + tbuf[part, 0]
+            second = second + tbuf[part, 1]
+            x = tbuf[part, 2]
+            continue
         packed = packed + tbuf[part, 0]
-        if j == T - 1:
-            x = tbuf[part, 1]
-            continue
         first = first + tbuf[part, 1] * x
         second = second + x * (tbuf[part, 2] + x * tbuf[part, 3])
         if j:
@@ -143,7 +152,7 @@
 
 def rows_sent(T, block):
     if block == T - 1:
-        return 2
+        return 3
     return 6 if block else 5
 
 
@@ -157,8 +166,9 @@
 
 
 def finish(T, E, rewards, s_buf, p_buf, carry_ref, ebuf, prior_ref, out_rewards, out_returns, out_stats,
-           rewards_out, returns_out, stats, sems):
+           both_out, stats, sems):
     chunk, _, lanes = rewards.shape
+    rewards_out, returns_out = both_out.at[0], both_out.at[1]
     entries = float(chunk * SUB * T * lanes * E)
     prior_count = entries
     half = lax.broadcasted_iota(jnp.int32, (1, lanes), 1) < lanes // 2
@@ -186,13 +196,12 @@
     send(returns_out, out_returns, 0)
     for k in range(chunk):
         rewards_out[k] = rewards[k] * inverse
-    send(rewards_out, out_rewards, 1)
+    send(rewards_out, out_rewards, 0)
     stats[0] = new_mean[0, 0]
     stats[1] = variance[0, 0]
-    last = pltpu.make_async_copy(stats, out_stats, sems.at[2])
+    last = pltpu.make_async_copy(stats, out_stats, sems.at[1])
     last.start()
-    pltpu.make_async_copy(returns_out, returns_out, sems.at[0]).wait()
-    pltpu.make_async_copy(rewards_out, rewards_out, sems.at[1]).wait()
+    pltpu.make_async_copy(both_out, both_out, sems.at[0]).wait()
     last.wait()
 
 
@@ -238,10 +247,9 @@
         in_specs=[vmem] * 6,
         out_specs=(hbm, hbm, hbm),
         scratch_shapes=[
-            pltpu.VMEM(steps, jnp.float32),
-            pltpu.VMEM(steps, jnp.float32),
+            pltpu.VMEM((2,) + steps, jnp.float32),
             pltpu.SMEM((2,), jnp.float32),
-            pltpu.SemaphoreType.DMA((3,)),
+            pltpu.SemaphoreType.DMA((2,)),
         ],
         compiler_params=pltpu.CompilerParams(vmem_limit_bytes=4 * 2**20),
     )(*between)

time: 11.3 us -> 11.3 us (level)
  no operation moved by 1% of the time
where the time goes in v5:
time: 11.3 us; the launch traced here: 11.1 us
  Pallas kernels  10.4 us (92%)
  between operations  0.66 us (6%)
    pallas_call x1, Pallas kernels, local(): exchange(rewards.reshape(split), dones.reshape(split), horizon.reshape(1,...  8.97 us
    pallas_call x1, Pallas kernels, local(): pl.pallas_call(functools.partial(finish, T, E), out_shape=(jax.ShapeDtype...  0.83 us
    pallas_call x1, Pallas kernels, local(): alone(mean)  0.65 us

profile of v5, /device:TPU:0, one launch (start us, length us, event | category | flops | bytes accessed | tf_op | source)
XLA Modules:
  0.0 11.1 jit_solution(961370109604790251)
XLA Ops:
  0.6 0.7 %conditional.1 = (f32[1,128]{1,0:T(1,128)S(1)}) conditional(s32[]{:T(128)} %clamp.3, () %tuple.20, (f32[1]{0:T(128)}) %tuple.23, (f32[1]{0:T(128)}) %tuple.24, () %tuple.21), branch_computations={%region_0.1_spmd, %region_1.2_spmd, %region_2.3_spmd, %region_3.4_... | conditional | bytes 524 | solution.py:237
  0.7 0.7 %branch_1_fun.1 = f32[1,128]{1,0:T(1,128)S(1)} custom-call(f32[1]{0:T(128)} %get-tuple-element.29.value), custom_call_target="tpu_custom_call" | custom-call | tf_op jit(solution)/shard_map/cond/branch_1_fun/pallas_call | solution.py:239
  1.3 9.0 %shard_map.93 = (f32[32,8,128]{2,1,0:T(8,128)S(1)}, f32[32,8,128]{2,1,0:T(8,128)S(1)}, f32[32,8,128]{2,1,0:T(8,128)S(1)}, f32[8,128]{1,0:T(8,128)S(1)}, f32[3,8,128]{2,1,0:T(8,128)S(1)}, /*index=5*/f32[2,128]{1,0:T(2,128)S(1)}) custom-call(f32[8,32,128]{2,1,0:T(8,128)} %bitcast.6, s32[8,32,128]{2,1,0:T(8,128)} %bitcast.7, f32[1,128]{1,0:T(1,128)} %bitcast.8, ...), custom_call_target="tpu_custom_call" | custom-call | tf_op jit(solution)/shard_map/pallas_call | solution.py:241
  10.3 0.8 %shard_map.94 = (f32[8,32,128]{2,1,0:T(8,128)}, f32[8,32,128]{2,1,0:T(8,128)}, f32[2]{0:T(128)}) custom-call(f32[32,8,128]{2,1,0:T(8,128)S(1)} %get-tuple-element.19.rewards, f32[32,8,128]{2,1,0:T(8,128)S(1)} %get-tuple-element.20.s_buf, f32[32,8,128]{2,1,0:T(8,128)S(1)} %get-tuple-element.21.p_buf, f32[8,128]{1,0:T(8,128)S(1)} %get-tuple-element.22.carry_ref, ...), custom_call_target="tpu_custom_call" | custom-call | tf_op jit(solution)/shard_map/pallas_call | solution.py:242

commit v6 on v5

--- a/solution.py
+++ b/solution.py
@@ -119,10 +119,10 @@
 
             lax.fori_loop(0, me, give, None)
             lax.fori_loop(me + 1, T * E, give, None)
+            left = measure.at[0:(T * E - 1) * count]
+            pltpu.make_async_copy(left, left, send_sem).wait()
             arrived = measure.at[0:total - count]
             pltpu.make_async_copy(arrived, arrived, recv_sem).wait()
-            left = measure.at[0:(T * E - 1) * count]
-            pltpu.make_async_copy(left, left, send_sem).wait()
 
     packed = jnp.zeros((E, lanes), jnp.float32)
     first = jnp.zeros((E, lanes), jnp.float32)

time: 11.3 us -> 11.3 us (level)
  no operation moved by 1% of the time
where the time goes in v6:
time: 11.3 us; the launch traced here: 11.1 us
  Pallas kernels  10.4 us (92%)
  between operations  0.66 us (6%)
    pallas_call x1, Pallas kernels, local(): exchange(rewards.reshape(split), dones.reshape(split), horizon.reshape(1,...  8.97 us
    pallas_call x1, Pallas kernels, local(): pl.pallas_call(functools.partial(finish, T, E), out_shape=(jax.ShapeDtype...  0.83 us
    pallas_call x1, Pallas kernels, local(): alone(mean)  0.65 us

profile of v6, /device:TPU:0, one launch (start us, length us, event | category | flops | bytes accessed | tf_op | source)
XLA Modules:
  0.0 11.1 jit_solution(16591343104889549416)
XLA Ops:
  0.6 0.7 %conditional.1 = (f32[1,128]{1,0:T(1,128)S(1)}) conditional(s32[]{:T(128)} %clamp.3, () %tuple.20, (f32[1]{0:T(128)}) %tuple.23, (f32[1]{0:T(128)}) %tuple.24, () %tuple.21), branch_computations={%region_0.1_spmd, %region_1.2_spmd, %region_2.3_spmd, %region_3.4_... | conditional | bytes 524 | solution.py:237
  0.7 0.7 %branch_1_fun.1 = f32[1,128]{1,0:T(1,128)S(1)} custom-call(f32[1]{0:T(128)} %get-tuple-element.29.value), custom_call_target="tpu_custom_call" | custom-call | tf_op jit(solution)/shard_map/cond/branch_1_fun/pallas_call | solution.py:239
  1.3 9.0 %shard_map.93 = (f32[32,8,128]{2,1,0:T(8,128)S(1)}, f32[32,8,128]{2,1,0:T(8,128)S(1)}, f32[32,8,128]{2,1,0:T(8,128)S(1)}, f32[8,128]{1,0:T(8,128)S(1)}, f32[3,8,128]{2,1,0:T(8,128)S(1)}, /*index=5*/f32[2,128]{1,0:T(2,128)S(1)}) custom-call(f32[8,32,128]{2,1,0:T(8,128)} %bitcast.6, s32[8,32,128]{2,1,0:T(8,128)} %bitcast.7, f32[1,128]{1,0:T(1,128)} %bitcast.8, ...), custom_call_target="tpu_custom_call" | custom-call | tf_op jit(solution)/shard_map/pallas_call | solution.py:241
  10.3 0.8 %shard_map.94 = (f32[8,32,128]{2,1,0:T(8,128)}, f32[8,32,128]{2,1,0:T(8,128)}, f32[2]{0:T(128)}) custom-call(f32[32,8,128]{2,1,0:T(8,128)S(1)} %get-tuple-element.19.rewards, f32[32,8,128]{2,1,0:T(8,128)S(1)} %get-tuple-element.20.s_buf, f32[32,8,128]{2,1,0:T(8,128)S(1)} %get-tuple-element.21.p_buf, f32[8,128]{1,0:T(8,128)S(1)} %get-tuple-element.22.carry_ref, ...), custom_call_target="tpu_custom_call" | custom-call | tf_op jit(solution)/shard_map/pallas_call | solution.py:242
